TPU v7x, 32 devices: a whole 2x2x4 slice. The times are simulated.
32 devices in a mesh: dp: 8 (over z, y), sub: 4 (over x, core).
Axes of the slice: x: 2, y: 2, z: 4, core: 2. Of those that a mesh axis runs over, the one named last changes fastest.
Arguments:
- embeddings: bfloat16 [16384, 1024], P(('dp', 'sub')), may hold values from -6 to 6
- rotation: bfloat16 [1024, 1024], replicated, may hold values from -0.1875 to 0.1875
- centroids: bfloat16 [8, 1024], replicated, may hold values from -6 to 6
- assignments: int32 [16384], P(('dp', 'sub')), may hold values from 0 to 7
- codes: int32 [16384, 64], P(('dp', 'sub')), may hold values from 0 to 255
Outputs:
- gram: float32 [1024, 1024], P('sub')
- coarse_sums: float32 [8, 1024], P('dp', 'sub')
- codebook_sums: float32 [256, 1024], P(None, 'sub')
All inputs are finite; a program needn't handle non-finite values.
Results may differ from a plain program's by a relative error of at most 0.0045.
Values may be sent and summed in bfloat16 or wider, within the bound.
A program may use at most 64 MiB of HBM per device.

v0:
```python
import jax
import jax.numpy as jnp
from jax import lax
from jax.sharding import PartitionSpec as P

D = 1024
M = 64
K = 256


def contract_rows(left, right):
    return lax.dot_general(
        left, right, (((0,), (0,)), ((), ())), preferred_element_type=jnp.float32
    )


def per_device(embeddings, rotation, centroids, assignments, codes):
    vec_rows, width = embeddings.shape
    cent_total = centroids.shape[0]
    sub_count = lax.axis_size("sub")
    dp_count = lax.axis_size("dp")
    total_rows = vec_rows * sub_count * dp_count
    columns = embeddings
    gram_part = lax.psum_scatter(
        contract_rows(columns, embeddings).astype(jnp.bfloat16),
        "sub",
        scatter_dimension=0,
        tiled=True,
    ).astype(jnp.float32)
    rotated = jnp.dot(embeddings, rotation, preferred_element_type=jnp.float32)
    labels = lax.broadcasted_iota(jnp.int32, (1, cent_total), 1)
    select = (assignments[:, None] == labels).astype(jnp.bfloat16)
    base = jnp.dot(select, centroids, preferred_element_type=jnp.float32)
    residual = (rotated - base).astype(jnp.bfloat16)
    onehot = (assignments[:, None] == lax.iota(jnp.int32, cent_total)[None, :]).astype(jnp.bfloat16)
    everything = contract_rows(onehot, residual)
    columns = lax.psum_scatter(
        everything.astype(jnp.bfloat16), "sub", scatter_dimension=1, tiled=True
    ).astype(jnp.float32)
    coarse = lax.psum_scatter(columns, "dp", scatter_dimension=0, tiled=True)
    coarse_sums = coarse * (cent_total / total_rows) ** 0.5
    code_words = codes.astype(jnp.bfloat16)
    moved, moved_codes = (
        lax.all_to_all(residual, "sub", split_axis=1, concat_axis=0, tiled=True),
        lax.all_to_all(code_words, "sub", split_axis=1, concat_axis=0, tiled=True),
    )
    local_m = codes.shape[1] // sub_count
    subw = D // M
    owner_codes = moved_codes.astype(jnp.int32)
    gathered_rows = moved.shape[0]
    words = lax.broadcasted_iota(jnp.int32, (1, 1, K), 2)
    onehot = (owner_codes[:, :, None] == words).astype(jnp.bfloat16)
    pieces = moved.reshape(gathered_rows, local_m, subw)
    book_blocks = jnp.einsum("rmk,rms->kms", onehot, pieces, preferred_element_type=jnp.float32)
    book_local = book_blocks.reshape(K, local_m * subw)
    gram_sum, book_sum = lax.psum((gram_part, book_local), "dp")
    gram = gram_sum / total_rows
    codebook_sums = book_sum * (K / total_rows) ** 0.5
    return (gram, coarse_sums, codebook_sums)


def solution(mesh):
    return jax.shard_map(
        per_device,
        mesh=mesh,
        in_specs=(P(("dp", "sub"), None), P(), P(), P(("dp", "sub")), P(("dp", "sub"), None)),
        out_specs=(P("sub", None), P("dp", "sub"), P(None, "sub")),
        check_vma=False,
    )
```

profile of v0, /device:TPU:0, one launch (start us, length us, event | category | flops | bytes accessed | tf_op | source)
XLA Modules:
  0.0 205.8 jit_solution(14390547988308779490)
XLA Ops:
  8.0 0.0 copy-start
  8.0 1.7 convert_element_type.39
  9.7 4.2 %all-to-all-start.1 = ((bf16[512,4,16]{0,2,1:T(8,128)(2,1)}), bf16[512,4,16]{0,2,1:T(8,128)(2,1)S(1)}, u32[]{:S(2)}, u32[]{:S(2)}) async-start(bf16[512,4,16]{0,2,1:T(8,128)(2,1)} %bitcast.1), calls=%async_computation.3 | async-start | bytes 131072 | tf_op jit(solution)/shard_map/all_to_all | solution.py:45
  13.9 0.0 copy-done
  13.9 0.0 copy-start.1
  14.0 2.5 %fusion.4 = f32[512,1024]{1,0:T(8,128)S(1)} fusion(bf16[512,1024]{1,0:T(8,128)(2,1)} %param.5, bf16[1024,1024]{1,0:T(8,128)(2,1)S(1)} %copy-done), kind=kOutput, calls=%fused_computation.14 | convolution fusion | flops 1073741824 | bytes 5242880 | tf_op jit(solution)/shard_map/dot_general | solution.py:30
  16.5 0.0 copy-done.1
  16.5 0.0 copy-done.2
  16.5 0.5 subtract_convert_fusion
  17.0 1.0 copy.20
  18.0 0.1 all-to-all-done.1
  18.1 4.2 %all-to-all-start = ((bf16[512,4,256]{2,0,1:T(8,128)(2,1)}), bf16[512,4,256]{2,0,1:T(8,128)(2,1)}, u32[]{:S(2)}, u32[]{:S(2)}) async-start(bf16[512,4,256]{2,0,1:T(8,128)(2,1)} %bitcast.24), calls=%async_computation.2 | async-start | bytes 2097152 | tf_op jit(solution)/shard_map/all_to_all | solution.py:44
  22.3 0.0 reduce-scatter.5.cloned.1.call-start
  22.4 1.0 convolution_convert_fusion.1
  23.4 0.0 reduce-scatter.5.cloned.1.call-update
  23.4 0.0 all-reduce.5.cloned.1.call-start
  23.5 13.3 %all-to-all-done = bf16[512,4,256]{2,0,1:T(8,128)(2,1)} async-done(((bf16[512,4,256]{2,0,1:T(8,128)(2,1)}), bf16[512,4,256]{2,0,1:T(8,128)(2,1)}, u32[]{:S(2)}, u32[]{:S(2)}) %all-to-all-start) | async-done | bytes 1048608 | tf_op jit(solution)/shard_map/all_to_all | solution.py:44
  36.8 1.9 copy.14
  38.7 1.6 reshape.27
  40.3 8.8 %fusion = f32[16,16,256]{2,1,0:T(8,128)S(1)} fusion(bf16[2048,16,16]{0,2,1:T(8,128)(2,1)} %reshape.27, s32[2048,16]{0,1:T(8,128)S(1)} %bitcast.26), kind=kOutput, calls=%fused_computation.1 | convolution fusion | flops 276824064 | bytes 1441792 | tf_op jit(solution)/shard_map/rmk,rms->kms/dot_general | solution.py:54
  49.1 0.8 copy.16
  49.9 0.0 all-reduce.5.cloned.1.call-update
  50.0 0.0 reduce-scatter.3.cloned.1.call-start
  50.0 4.2 %convolution_convert_fusion = bf16[1024,1024]{1,0:T(8,128)(2,1)} fusion(bf16[512,1024]{1,0:T(8,128)(2,1)} %param.5), kind=kOutput, calls=%fused_computation.4 | convolution fusion | flops 1074790400 | bytes 3145728 | tf_op jit(solution)/shard_map/dot_general | solution.py:12
  54.2 0.0 reduce-scatter.3.cloned.1.call-update
  54.3 0.6 copy-done.3
  54.9 0.6 dynamic-slice
  55.5 66.0 %all-reduce.5.cloned.1.call-done = f32[256,256]{1,0:T(8,128)} async-done(((f32[256,256]{1,0:T(8,128)}), f32[256,256]{1,0:T(8,128)}) %all-reduce.5.cloned.1.call-update) | async-done | bytes 262160 | tf_op jit(solution)/shard_map/psum | solution.py:56
  121.5 1.7 broadcast_multiply_fusion.1
  123.2 73.0 %all-reduce.6 = (f32[256,1024]{1,0:T(8,128)S(1)}, f32[8,256]{1,0:T(8,128)S(1)}) all-reduce(bf16[256,1024]{1,0:T(8,128)(2,1)} %reduce-scatter.3.cloned.1.call-done, bf16[8,256]{1,0:T(8,128)(2,1)} %reduce-scatter.5.cloned.1.call-done), channel_id=1, replica_groups=mesh['dp'=8,'sub'=4] {'dp'}, use_global_device_ids=true, to_apply=%region_1.0 | all-reduce | flops 264192 | bytes 1585152 | tf_op jit(solution)/shard_map/psum | solution.py:56
  196.2 1.1 broadcast_multiply_fusion
  197.2 1.2 dynamic-slice_multiply_fusion
  (6 shorter events, 0.0 us)
Async XLA Ops:
  8.0 5.9 %copy-start = (bf16[1024,1024]{1,0:T(8,128)(2,1)S(1)}, bf16[1024,1024]{1,0:T(8,128)(2,1)}, u32[]{:S(2)}) copy-start(bf16[1024,1024]{1,0:T(8,128)(2,1)} %param.6) | copy-start | bytes 6291460
  9.7 8.4 %all-to-all-start.1 = ((bf16[512,4,16]{0,2,1:T(8,128)(2,1)}), bf16[512,4,16]{0,2,1:T(8,128)(2,1)S(1)}, u32[]{:S(2)}, u32[]{:S(2)}) async-start(bf16[512,4,16]{0,2,1:T(8,128)(2,1)} %bitcast.1), calls=%async_computation.3 | async-start | bytes 131072 | tf_op jit(solution)/shard_map/all_to_all | solution.py:45
  13.9 2.5 %copy-start.1 = (bf16[8,1024]{1,0:T(8,128)(2,1)S(1)}, bf16[8,1024]{1,0:T(8,128)(2,1)}, u32[]{:S(2)}) copy-start(bf16[8,1024]{1,0:T(8,128)(2,1)} %param.7) | copy-start | bytes 49156
  13.9 2.5 %copy-start.2 = (s32[512]{0:T(512)S(1)}, s32[512]{0:T(512)}, u32[]{:S(2)}) copy-start(s32[512]{0:T(512)} %param.8) | copy-start | bytes 6148
  18.1 18.7 %all-to-all-start = ((bf16[512,4,256]{2,0,1:T(8,128)(2,1)}), bf16[512,4,256]{2,0,1:T(8,128)(2,1)}, u32[]{:S(2)}, u32[]{:S(2)}) async-start(bf16[512,4,256]{2,0,1:T(8,128)(2,1)} %bitcast.24), calls=%async_computation.2 | async-start | bytes 2097152 | tf_op jit(solution)/shard_map/all_to_all | solution.py:44
  22.3 33.2 %reduce-scatter.5.cloned.1.call-start = ((), (), s32[]{:S(2)}) async-start(), calls=%async_computation.5 | async-start | bytes 20480 | tf_op jit(solution)/shard_map/reduce_scatter | solution.py:37
  23.4 98.1 %all-reduce.5.cloned.1.call-start = ((), (), s32[]{:S(2)}) async-start(), calls=%async_computation.6 | async-start | bytes 524288 | tf_op jit(solution)/shard_map/psum | solution.py:56
  50.0 73.2 %reduce-scatter.3.cloned.1.call-start = ((), (), s32[]{:S(2)}) async-start(), calls=%async_computation.4 | async-start | bytes 2621440 | tf_op jit(solution)/shard_map/reduce_scatter | solution.py:24
  54.2 0.7 copy-start.3
Sparse Core Ops, SparseCore 0:
  25.5 21.7 reduce-scatter.4
  54.4 31.9 reduce-scatter.2
Sparse Core Ops, SparseCore 1:
  50.1 71.4 all-reduce.4
where the time goes:
time: 206 us
  waiting for transfers between devices  79.4 us (39%)
  blocking collectives  73 us (35%)
  matrix products  17 us (8%)
  between operations  15.6 us (8%)
  starting transfers between devices  8.61 us (4%)
  local copies, waits for them, and re-layouts  6.58 us (3%)
  other arithmetic  5.62 us (3%)
    psum x1, blocking collectives, per_device(): gram_sum, book_sum = lax.psum((gram_part, book_local), 'dp')  73 us
    psum x1, waiting for transfers between devices, per_device(): gram_sum, book_sum = lax.psum((gram_part, book_local), 'dp')  66 us
    all_to_all x1, waiting for transfers between devices, per_device(): lax.all_to_all(residual, 'sub', split_axis=1, concat_axis=0, tiled=True)  13.3 us
    dot_general x1, matrix products, per_device(): jnp.einsum('rmk,rms->kms', onehot, pieces, preferred_element_type=jnp.flo...  8.83 us
    dot_general x2, matrix products, contract_rows(): lax.dot_general(left, right, (((0,), (0,)), ((), ())), preferred_element_...  5.23 us
    all_to_all x1, starting transfers between devices, per_device(): lax.all_to_all(residual, 'sub', split_axis=1, concat_axis=0, tiled=True)  4.25 us
    all_to_all x1, starting transfers between devices, per_device(): lax.all_to_all(code_words, 'sub', split_axis=1, concat_axis=0, tiled=True)  4.24 us
  transfers between devices with their start and end apart: 5, of which 3 were waited for; matrix products, arithmetic and copies ran while one was open for 12% of the time, Pallas kernels for 0%

commit v1 on v0

--- a/solution.py
+++ b/solution.py
@@ -1,11 +1,16 @@
+import functools
+
 import jax
 import jax.numpy as jnp
 from jax import lax
+from jax.experimental import pallas as pl
+from jax.experimental.pallas import tpu as pltpu
 from jax.sharding import PartitionSpec as P
 
-D = 1024
 M = 64
 K = 256
+LANES = 128
+PIECES = 2
 
 
 def contract_rows(left, right):
@@ -14,15 +19,14 @@
     )
 
 
-def per_device(embeddings, rotation, centroids, assignments, codes):
+def plain_per_device(embeddings, rotation, centroids, assignments, codes):
     vec_rows, width = embeddings.shape
     cent_total = centroids.shape[0]
     sub_count = lax.axis_size("sub")
     dp_count = lax.axis_size("dp")
     total_rows = vec_rows * sub_count * dp_count
-    columns = embeddings
     gram_part = lax.psum_scatter(
-        contract_rows(columns, embeddings).astype(jnp.bfloat16),
+        contract_rows(embeddings, embeddings).astype(jnp.bfloat16),
         "sub",
         scatter_dimension=0,
         tiled=True,
@@ -32,8 +36,7 @@
     select = (assignments[:, None] == labels).astype(jnp.bfloat16)
     base = jnp.dot(select, centroids, preferred_element_type=jnp.float32)
     residual = (rotated - base).astype(jnp.bfloat16)
-    onehot = (assignments[:, None] == lax.iota(jnp.int32, cent_total)[None, :]).astype(jnp.bfloat16)
-    everything = contract_rows(onehot, residual)
+    everything = contract_rows(select, residual)
     columns = lax.psum_scatter(
         everything.astype(jnp.bfloat16), "sub", scatter_dimension=1, tiled=True
     ).astype(jnp.float32)
@@ -45,7 +48,7 @@
         lax.all_to_all(code_words, "sub", split_axis=1, concat_axis=0, tiled=True),
     )
     local_m = codes.shape[1] // sub_count
-    subw = D // M
+    subw = width // codes.shape[1]
     owner_codes = moved_codes.astype(jnp.int32)
     gathered_rows = moved.shape[0]
     words = lax.broadcasted_iota(jnp.int32, (1, 1, K), 2)
@@ -59,7 +62,270 @@
     return (gram, coarse_sums, codebook_sums)
 
 
+def kernel(
+    ns, nd, total_rows,
+    emb, rot, cent, asg, codes,
+    gram_o, coarse_o, book_o,
+    gs1, gr1, gs2, gr2, gacc, gs3, gr3, gag,
+    res, codes_t, ball, br1, bs2, br2, bacc, bs3, br3, bag, cs3, cr3,
+    ssem, rsem,
+):
+    rows, width = emb.shape
+    cents = cent.shape[0]
+    nh = ns // 2
+    gr = width // ns
+    pr = gr // PIECES
+    cr = pr // nd
+    bc = width // ns
+    kr = K // nd
+    f32, bf16 = jnp.float32, jnp.bfloat16
+    d = lax.axis_index("dp")
+    s = lax.axis_index("sub")
+    half, par = s // 2, lax.rem(s, 2)
+    other = 1 - par
+    pair = (d, half * 2 + other)
+
+    def mate(k):
+        return lax.rem(half + k, nh)
+
+    def peer(k):
+        return lax.rem(d + k, nd)
+
+    barrier = pltpu.get_barrier_semaphore()
+    greet = [pair]
+    greet += [(d, mate(k) * 2 + par) for k in range(1, nh)]
+    greet += [(peer(k), s) for k in range(1, nd)]
+    for who in greet:
+        pl.semaphore_signal(barrier, inc=1, device_id=who, device_id_type=pl.DeviceIdType.MESH)
+
+    started = []
+
+    def send(src, dst, who):
+        n = len(started)
+        copy = pltpu.make_async_remote_copy(
+            src_ref=src, dst_ref=dst, send_sem=ssem.at[n], recv_sem=rsem.at[n],
+            device_id=who, device_id_type=pl.DeviceIdType.MESH,
+        )
+        copy.start()
+        started.append(copy)
+        return copy
+
+    def gram_block(q):
+        cols = pl.ds(pl.multiple_of(q * gr, gr), gr)
+        return contract_rows(emb[:, cols], emb[...]).astype(bf16)
+
+    first = []
+    for k in range(nh):
+        i = mate(nh - 1 - k)
+        gs1[k] = gram_block(i * 2 + other)
+        if k == 0:
+            pl.semaphore_wait(barrier, len(greet))
+        first.append(send(gs1.at[k], gr1.at[k], pair))
+    g2 = {}
+    for k in range(nh):
+        i = mate(nh - 1 - k)
+        own = gram_block(i * 2 + par)
+        first[k].wait_recv()
+        both = own.astype(f32) + gr1[k].astype(f32)
+        if k < nh - 1:
+            gs2[k] = both.astype(bf16)
+            who = (d, i * 2 + par)
+            for h in range(PIECES):
+                span = pl.ds(h * pr, pr)
+                g2[k, h] = send(gs2.at[k, span], gr2.at[k, span], who)
+        else:
+            gacc[...] = both
+
+    asg_row = asg[...]
+    select = (asg_row == lax.broadcasted_iota(jnp.int32, (cents, rows), 0)).astype(f32).astype(bf16)
+    for c in range(width // 256):
+        cols = slice(c * 256, (c + 1) * 256)
+        rotated = jnp.dot(emb[...], rot[:, cols], preferred_element_type=f32)
+        base = contract_rows(select, cent[:, cols])
+        res[:, cols] = (rotated - base).astype(bf16)
+    m = codes.shape[1]
+    eye = (
+        lax.broadcasted_iota(jnp.int32, (m, m), 0) == lax.broadcasted_iota(jnp.int32, (m, m), 1)
+    ).astype(f32).astype(bf16)
+    codes_t[...] = lax.dot_general(
+        eye, codes[...].astype(f32).astype(bf16), (((1,), (1,)), ((), ())),
+        preferred_element_type=f32,
+    ).astype(jnp.int32)
+
+    subw = width // m
+    per = LANES // subw
+    lane_owner = lax.broadcasted_iota(jnp.int32, (K, LANES), 1) // subw
+    words = lax.broadcasted_iota(jnp.int32, (K, rows), 0)
+    groups = bc // LANES
+
+    def group_step(g, carry):
+        q, off = g // groups, lax.rem(g, groups)
+        part = res[:, pl.ds(pl.multiple_of(g * LANES, LANES), LANES)]
+        names = codes_t[pl.ds(pl.multiple_of(g * per, per), per), :]
+        total = jnp.zeros((K, LANES), f32)
+        for j in range(per):
+            hot = jnp.where(names[j : j + 1, :] == words, 1.0, 0.0).astype(bf16)
+            got = jnp.dot(hot, part, preferred_element_type=f32)
+            total = jnp.where(lane_owner == j, got, total)
+        lanes = pl.ds(pl.multiple_of(off * LANES, LANES), LANES)
+        ball[q, 0:K, lanes] = total
+        return carry
+
+    lax.fori_loop(0, width // LANES, group_step, 0)
+    cpad = ball.shape[1] - K
+    select_pad = (asg_row == lax.broadcasted_iota(jnp.int32, (cpad, rows), 0)).astype(f32).astype(bf16)
+    for q in range(ns):
+        ball[q, K : K + cpad, :] = jnp.dot(
+            select_pad, res[:, q * bc : (q + 1) * bc], preferred_element_type=f32
+        )
+
+    b1 = []
+    for k in range(nh):
+        i = mate(nh - 1 - k)
+        b1.append(send(ball.at[i * 2 + other], br1.at[k], pair))
+    b2 = {}
+    for k in range(nh):
+        i = mate(nh - 1 - k)
+        b1[k].wait_recv()
+        both = ball[i * 2 + par] + br1[k]
+        if k < nh - 1:
+            bs2[k] = both.astype(bf16)
+            b2[k] = send(bs2.at[k], br2.at[k], (d, i * 2 + par))
+        else:
+            bacc[...] = both
+
+    g3 = {}
+    for h in range(PIECES):
+        span = pl.ds(h * pr, pr)
+        total = gacc[span, :]
+        for k in range(nh - 1):
+            g2[k, h].wait_recv()
+            total = total + gr2[k, span, :].astype(f32)
+        gacc[span, :] = total
+        gs3[h] = total.astype(bf16).reshape(nd, cr, width)
+        for k in range(1, nd):
+            g3[h, k] = send(gs3.at[h, peer(k)], gr3.at[h, k - 1], (peer(k), s))
+    total = bacc[...]
+    for k in range(nh - 1):
+        b2[k].wait_recv()
+        total = total + br2[k].astype(f32)
+    bs3[...] = total[0:K].reshape(nd, kr, bc)
+    cper = cents // nd
+    for e in range(nd):
+        cs3[e] = total[K + e * cper : K + (e + 1) * cper]
+    b3, c3 = {}, {}
+    for k in range(1, nd):
+        b3[k] = send(bs3.at[peer(k)], br3.at[k - 1], (peer(k), s))
+        c3[k] = send(cs3.at[peer(k)], cr3.at[k - 1], (peer(k), s))
+
+    g4 = {}
+    for h in range(PIECES):
+        total = gacc[pl.ds(pl.multiple_of(h * pr + d * cr, cr), cr), :]
+        for k in range(1, nd):
+            g3[h, k].wait_recv()
+            total = total + gr3[h, k - 1].astype(f32)
+        gag[h, d] = total.astype(bf16)
+        for k in range(1, nd):
+            g4[h, k] = send(gag.at[h, d], gag.at[h, d], (peer(k), s))
+    total = bs3[d]
+    ctotal = cs3[d]
+    for k in range(1, nd):
+        b3[k].wait_recv()
+        c3[k].wait_recv()
+        total = total + br3[k - 1]
+        ctotal = ctotal + cr3[k - 1]
+    bag[d] = total.astype(bf16)
+    b4 = {}
+    for k in range(1, nd):
+        b4[k] = send(bag.at[d], bag.at[d], (peer(k), s))
+    coarse_o[...] = ctotal * (cents / total_rows) ** 0.5
+    for h in range(PIECES):
+        for k in range(1, nd):
+            g4[h, k].wait_recv()
+        gram_o[h * pr : (h + 1) * pr, :] = gag[h].astype(f32).reshape(pr, width) * (1.0 / total_rows)
+    for k in range(1, nd):
+        b4[k].wait_recv()
+    book_o[...] = bag[...].astype(f32).reshape(K, bc) * (K / total_rows) ** 0.5
+    for copy in started:
+        copy.wait_send()
+
+
+def fused_per_device(ns, nd, embeddings, rotation, centroids, assignments, codes):
+    rows, width = embeddings.shape
+    cents = centroids.shape[0]
+    total_rows = rows * ns * nd
+    nh = ns // 2
+    gr = width // ns
+    pr = gr // PIECES
+    cr = pr // nd
+    bc = width // ns
+    cpad = -(-cents // 16) * 16
+    f32, bf16 = jnp.float32, jnp.bfloat16
+    far = max(nh - 1, 1)
+    copies = nh + (nh - 1) * PIECES + nh + (nh - 1) + (nd - 1) * (2 * PIECES + 3)
+    scratch = [
+        pltpu.VMEM((nh, gr, width), bf16),
+        pltpu.VMEM((nh, gr, width), bf16),
+        pltpu.VMEM((far, gr, width), bf16),
+        pltpu.VMEM((far, gr, width), bf16),
+        pltpu.VMEM((gr, width), f32),
+        pltpu.VMEM((PIECES, nd, cr, width), bf16),
+        pltpu.VMEM((PIECES, nd - 1, cr, width), bf16),
+        pltpu.VMEM((PIECES, nd, cr, width), bf16),
+        pltpu.VMEM((rows, width), bf16),
+        pltpu.VMEM((codes.shape[1], rows), jnp.int32),
+        pltpu.VMEM((ns, K + cpad, bc), f32),
+        pltpu.VMEM((nh, K + cpad, bc), f32),
+        pltpu.VMEM((far, K + cpad, bc), bf16),
+        pltpu.VMEM((far, K + cpad, bc), bf16),
+        pltpu.VMEM((K + cpad, bc), f32),
+        pltpu.VMEM((nd, K // nd, bc), f32),
+        pltpu.VMEM((nd - 1, K // nd, bc), f32),
+        pltpu.VMEM((nd, K // nd, bc), bf16),
+        pltpu.VMEM((nd, cents // nd, bc), f32),
+        pltpu.VMEM((nd - 1, cents // nd, bc), f32),
+        pltpu.SemaphoreType.DMA((copies,)),
+        pltpu.SemaphoreType.DMA((copies,)),
+    ]
+    vmem = pl.BlockSpec(memory_space=pltpu.VMEM)
+    return tuple(
+        pl.pallas_call(
+            functools.partial(kernel, ns, nd, total_rows),
+            out_shape=(
+                jax.ShapeDtypeStruct((gr, width), f32),
+                jax.ShapeDtypeStruct((cents // nd, bc), f32),
+                jax.ShapeDtypeStruct((K, bc), f32),
+            ),
+            in_specs=[vmem] * 5,
+            out_specs=(vmem,) * 3,
+            scratch_shapes=scratch,
+            compiler_params=pltpu.CompilerParams(
+                collective_id=0, has_side_effects=True, vmem_limit_bytes=56 * 1024 * 1024
+            ),
+        )(embeddings, rotation, centroids, assignments.reshape(1, rows), codes)
+    )
+
+
 def solution(mesh):
+    ns, nd = mesh.shape["sub"], mesh.shape["dp"]
+
+    def per_device(embeddings, rotation, centroids, assignments, codes):
+        rows, width = embeddings.shape
+        cents = centroids.shape[0]
+        fits = (
+            ns % 2 == 0
+            and nd > 1
+            and width % (ns * PIECES * nd * 16) == 0
+            and width % (ns * 2 * LANES // 2) == 0
+            and K % (nd * 16) == 0
+            and cents % nd == 0
+            and cents % 8 == 0
+            and LANES % (width // M) == 0
+        )
+        if fits:
+            return fused_per_device(ns, nd, embeddings, rotation, centroids, assignments, codes)
+        return plain_per_device(embeddings, rotation, centroids, assignments, codes)
+
     return jax.shard_map(
         per_device,
         mesh=mesh,

time: 206 us -> 59.8 us (0.29)
  waiting for transfers between devices: 79.4 us -> 0 us
  blocking collectives: 73 us -> 0 us
  Pallas kernels: 0 us -> 53.6 us
  matrix products: 17 us -> 0 us
  between operations: 15.6 us -> 0.66 us
  starting transfers between devices: 8.61 us -> 0 us
  other arithmetic: 5.62 us -> 0 us
    psum x1 -> x0, blocking collectives: 73 us -> none  [per_device(): gram_sum, book_sum = lax.psum((gram_part, book_local), 'dp')]
    psum x1 -> x0, waiting for transfers between devices: 66 us -> none  [per_device(): gram_sum, book_sum = lax.psum((gram_part, book_local), 'dp')]
    pallas_call x0 -> x1, Pallas kernels: none -> 53.6 us  [fused_per_device(): pl.pallas_call(functools.partial(kernel, ns, nd, total_rows), out_shape=(...]
    dot_general x5 -> x0, matrix products: 17 us -> none  [the longest x1 8.83 us: per_device(): jnp.einsum('rmk,rms->kms', onehot, pieces, preferred_element_type=jnp.flo...]
    all_to_all x2 -> x0, waiting for transfers between devices: 13.4 us -> none  [the longest x1 13.3 us: per_device(): lax.all_to_all(residual, 'sub', split_axis=1, concat_axis=0, tiled=True)]
    all_to_all x2 -> x0, starting transfers between devices: 8.48 us -> none  [the longest x1 4.25 us: per_device(): lax.all_to_all(residual, 'sub', split_axis=1, concat_axis=0, tiled=True)]
    unnamed x9 -> x8, local copies, waits for them, and re-layouts: 1.24 us -> 5.36 us
    all_to_all x2 -> x0, local copies, waits for them, and re-layouts: 2.9 us -> none  [per_device(): lax.all_to_all(residual, 'sub', split_axis=1, concat_axis=0, tiled=True)]
  transfers between devices with their start and end apart: 5 -> 0, of which waited for: 3 -> 0; matrix products, arithmetic and copies ran while one was open for 12% -> 0% of each run, Pallas kernels for 0% -> 0%
where the time goes in v1:
time: 59.8 us; the launch traced here: 59.6 us
  Pallas kernels  53.6 us (90%)
  local copies, waits for them, and re-layouts  5.36 us (9%)
  between operations  0.66 us (1%)
    pallas_call x1, Pallas kernels, fused_per_device(): pl.pallas_call(functools.partial(kernel, ns, nd, total_rows), out_shape=(...  53.6 us
    unnamed x8, local copies, waits for them, and re-layouts  5.36 us

profile of v1, /device:TPU:0, one launch (start us, length us, event | category | flops | bytes accessed | tf_op | source)
XLA Modules:
  0.0 59.6 jit_solution(14284184416460581135)
XLA Ops:
  0.6 1.7 %copy.8.codes = s32[512,64]{1,0:T(8,128)} copy(s32[512,64]{0,1:T(8,128)} %param.9) | data formatting | bytes 262144 | tf_op args[4]
  2.4 53.6 %shard_map.76 = (f32[256,1024]{1,0:T(8,128)}, f32[1,256]{1,0:T(1,128)}, f32[256,256]{1,0:T(8,128)}) custom-call(bf16[512,1024]{1,0:T(8,128)(2,1)} %emb.1, bf16[1024,1024]{1,0:T(8,128)(2,1)} %rot.1, bf16[8,1024]{1,0:T(8,128)(2,1)} %cent.1, s32[1,512]{1,0:T(1,128)} %bitcast.1, s32[512,64]{1,0:T(8,128)} %copy.8.codes), custom_call_target="tpu_custom_call" | custom-call | tf_op jit(solution)/shard_map/pallas_call | solution.py:292
  55.9 0.0 copy-start.1
  56.0 0.0 copy-start
  56.0 2.3 %copy.12 = f32[256,1024]{1,0:T(8,128)} copy(f32[256,1024]{1,0:T(8,128)} %get-tuple-element.6) | data formatting | bytes 2097152
  58.3 0.0 copy-done.1
  58.3 0.6 copy.13
  58.9 0.0 copy-done
  58.9 0.7 %copy.14 = f32[256,256]{1,0:T(8,128)} copy(f32[256,256]{1,0:T(8,128)S(1)} %copy-done) | data formatting | bytes 524288
Async XLA Ops:
  55.9 2.4 %copy-start.1 = (f32[1,256]{1,0:T(1,128)S(1)}, f32[1,256]{1,0:T(1,128)}, u32[]{:S(2)}) copy-start(f32[1,256]{1,0:T(1,128)} %get-tuple-element.7) | copy-start | bytes 3076
  56.0 2.9 %copy-start = (f32[256,256]{1,0:T(8,128)S(1)}, f32[256,256]{1,0:T(8,128)}, u32[]{:S(2)}) copy-start(f32[256,256]{1,0:T(8,128)} %get-tuple-element.8) | copy-start | bytes 786436

commit v2 on v1

--- a/solution.py
+++ b/solution.py
@@ -66,8 +66,8 @@
     ns, nd, total_rows,
     emb, rot, cent, asg, codes,
     gram_o, coarse_o, book_o,
-    gs1, gr1, gs2, gr2, gacc, gs3, gr3, gag,
-    res, codes_t, ball, br1, bs2, br2, bacc, bs3, br3, bag, cs3, cr3,
+    gs1, gr1, gs2, gr2, gacc, gx, gs3, gr3, gy, gs4, gr4, gag,
+    res, codes_t, ball, br1, bs2, br2, bacc, bs3, br3, bs4, br4, bag, cs3, cr3,
     ssem, rsem,
 ):
     rows, width = emb.shape
@@ -82,6 +82,8 @@
     d = lax.axis_index("dp")
     s = lax.axis_index("sub")
     half, par = s // 2, lax.rem(s, 2)
+    nq = nd // 2
+    dq, dpar = d // 2, lax.rem(d, 2)
     other = 1 - par
     pair = (d, half * 2 + other)
 
@@ -194,6 +196,10 @@
         else:
             bacc[...] = both
 
+    def quarter(k):
+        return lax.rem(dq + k, nq)
+
+    partner = (dq * 2 + 1 - dpar, s)
     g3 = {}
     for h in range(PIECES):
         span = pl.ds(h * pr, pr)
@@ -201,50 +207,78 @@
         for k in range(nh - 1):
             g2[k, h].wait_recv()
             total = total + gr2[k, span, :].astype(f32)
-        gacc[span, :] = total
-        gs3[h] = total.astype(bf16).reshape(nd, cr, width)
-        for k in range(1, nd):
-            g3[h, k] = send(gs3.at[h, peer(k)], gr3.at[h, k - 1], (peer(k), s))
+        split = total.reshape(nq, 2, cr, width)
+        for e in range(2):
+            gx[h, e] = split[:, e]
+            gs3[h, e] = split[:, e].astype(bf16)
+        g3[h] = send(gs3.at[h, 1 - dpar], gr3.at[h], partner)
     total = bacc[...]
     for k in range(nh - 1):
         b2[k].wait_recv()
         total = total + br2[k].astype(f32)
-    bs3[...] = total[0:K].reshape(nd, kr, bc)
+    split = total[0:K].reshape(nq, 2, kr, bc)
+    for e in range(2):
+        bs3[e] = split[:, e]
+    b3 = send(bs3.at[1 - dpar], br3, partner)
     cper = cents // nd
     for e in range(nd):
         cs3[e] = total[K + e * cper : K + (e + 1) * cper]
-    b3, c3 = {}, {}
+    c3 = {}
     for k in range(1, nd):
-        b3[k] = send(bs3.at[peer(k)], br3.at[k - 1], (peer(k), s))
         c3[k] = send(cs3.at[peer(k)], cr3.at[k - 1], (peer(k), s))
 
     g4 = {}
     for h in range(PIECES):
-        total = gacc[pl.ds(pl.multiple_of(h * pr + d * cr, cr), cr), :]
-        for k in range(1, nd):
-            g3[h, k].wait_recv()
-            total = total + gr3[h, k - 1].astype(f32)
+        g3[h].wait_recv()
+        total = gx[h, dpar] + gr3[h].astype(f32)
+        gy[h] = total
+        gs4[h] = total.astype(bf16)
+        for k in range(1, nq):
+            g4[h, k] = send(gs4.at[h, quarter(k)], gr4.at[h, k - 1], (quarter(k) * 2 + dpar, s))
+    b3.wait_recv()
+    bs4[...] = bs3[dpar] + br3[...]
+    b4 = {}
+    for k in range(1, nq):
+        b4[k] = send(bs4.at[quarter(k)], br4.at[k - 1], (quarter(k) * 2 + dpar, s))
+
+    g5, b5 = {}, {}
+    for h in range(PIECES):
+        total = gy[h, dq]
+        for k in range(1, nq):
+            g4[h, k].wait_recv()
+            total = total + gr4[h, k - 1].astype(f32)
         gag[h, d] = total.astype(bf16)
-        for k in range(1, nd):
-            g4[h, k] = send(gag.at[h, d], gag.at[h, d], (peer(k), s))
-    total = bs3[d]
+        for k in range(1, nq):
+            g5[h, k] = send(gag.at[h, d], gag.at[h, d], (quarter(k) * 2 + dpar, s))
+        g5[h, 0, "y"] = send(gag.at[h, d], gag.at[h, d], partner)
+    total = bs4[dq]
+    for k in range(1, nq):
+        b4[k].wait_recv()
+        total = total + br4[k - 1]
+    bag[d] = total.astype(bf16)
+    for k in range(1, nq):
+        b5[k] = send(bag.at[d], bag.at[d], (quarter(k) * 2 + dpar, s))
+    b5[0, "y"] = send(bag.at[d], bag.at[d], partner)
+    for h in range(PIECES):
+        for k in range(1, nq):
+            g5[h, k].wait_recv()
+            slot = quarter(nq - k) * 2 + dpar
+            g5[h, k, "y"] = send(gag.at[h, slot], gag.at[h, slot], partner)
+    for k in range(1, nq):
+        b5[k].wait_recv()
+        slot = quarter(nq - k) * 2 + dpar
+        b5[k, "y"] = send(bag.at[slot], bag.at[slot], partner)
     ctotal = cs3[d]
     for k in range(1, nd):
-        b3[k].wait_recv()
         c3[k].wait_recv()
-        total = total + br3[k - 1]
         ctotal = ctotal + cr3[k - 1]
-    bag[d] = total.astype(bf16)
-    b4 = {}
-    for k in range(1, nd):
-        b4[k] = send(bag.at[d], bag.at[d], (peer(k), s))
     coarse_o[...] = ctotal * (cents / total_rows) ** 0.5
     for h in range(PIECES):
-        for k in range(1, nd):
-            g4[h, k].wait_recv()
+        for k in range(nq):
+            g5[h, k, "y"].wait_recv()
         gram_o[h * pr : (h + 1) * pr, :] = gag[h].astype(f32).reshape(pr, width) * (1.0 / total_rows)
-    for k in range(1, nd):
-        b4[k].wait_recv()
+    for k in range(nq):
+        b5[k, "y"].wait_recv()
     book_o[...] = bag[...].astype(f32).reshape(K, bc) * (K / total_rows) ** 0.5
     for copy in started:
         copy.wait_send()
@@ -262,15 +296,21 @@
     cpad = -(-cents // 16) * 16
     f32, bf16 = jnp.float32, jnp.bfloat16
     far = max(nh - 1, 1)
-    copies = nh + (nh - 1) * PIECES + nh + (nh - 1) + (nd - 1) * (2 * PIECES + 3)
+    nq = nd // 2
+    kr = K // nd
+    copies = nh + (nh - 1) * PIECES + nh + (nh - 1) + (PIECES + 1) * (3 * nq - 1) + nd - 1
     scratch = [
         pltpu.VMEM((nh, gr, width), bf16),
         pltpu.VMEM((nh, gr, width), bf16),
         pltpu.VMEM((far, gr, width), bf16),
         pltpu.VMEM((far, gr, width), bf16),
         pltpu.VMEM((gr, width), f32),
-        pltpu.VMEM((PIECES, nd, cr, width), bf16),
-        pltpu.VMEM((PIECES, nd - 1, cr, width), bf16),
+        pltpu.VMEM((PIECES, 2, nq, cr, width), f32),
+        pltpu.VMEM((PIECES, 2, nq, cr, width), bf16),
+        pltpu.VMEM((PIECES, nq, cr, width), bf16),
+        pltpu.VMEM((PIECES, nq, cr, width), f32),
+        pltpu.VMEM((PIECES, nq, cr, width), bf16),
+        pltpu.VMEM((PIECES, nq - 1, cr, width), bf16),
         pltpu.VMEM((PIECES, nd, cr, width), bf16),
         pltpu.VMEM((rows, width), bf16),
         pltpu.VMEM((codes.shape[1], rows), jnp.int32),
@@ -279,8 +319,10 @@
         pltpu.VMEM((far, K + cpad, bc), bf16),
         pltpu.VMEM((far, K + cpad, bc), bf16),
         pltpu.VMEM((K + cpad, bc), f32),
-        pltpu.VMEM((nd, K // nd, bc), f32),
-        pltpu.VMEM((nd - 1, K // nd, bc), f32),
+        pltpu.VMEM((2, nq, kr, bc), f32),
+        pltpu.VMEM((nq, kr, bc), f32),
+        pltpu.VMEM((nq, kr, bc), f32),
+        pltpu.VMEM((nq - 1, kr, bc), f32),
         pltpu.VMEM((nd, K // nd, bc), bf16),
         pltpu.VMEM((nd, cents // nd, bc), f32),
         pltpu.VMEM((nd - 1, cents // nd, bc), f32),
@@ -314,7 +356,8 @@
         cents = centroids.shape[0]
         fits = (
             ns % 2 == 0
-            and nd > 1
+            and nd > 2
+            and nd % 2 == 0
             and width % (ns * PIECES * nd * 16) == 0
             and width % (ns * 2 * LANES // 2) == 0
             and K % (nd * 16) == 0

time: 59.8 us -> 54.1 us (0.905)
  Pallas kernels: 53.6 us -> 48 us
    pallas_call x1, Pallas kernels: 53.6 us -> 48 us  [fused_per_device(): pl.pallas_call(functools.partial(kernel, ns, nd, total_rows), out_shape=(...]
where the time goes in v2:
time: 54.1 us; the launch traced here: 54 us
  Pallas kernels  48 us (89%)
  local copies, waits for them, and re-layouts  5.36 us (10%)
  between operations  0.66 us (1%)
    pallas_call x1, Pallas kernels, fused_per_device(): pl.pallas_call(functools.partial(kernel, ns, nd, total_rows), out_shape=(...  48 us
    unnamed x8, local copies, waits for them, and re-layouts  5.36 us

profile of v2, /device:TPU:0, one launch (start us, length us, event | category | flops | bytes accessed | tf_op | source)
XLA Modules:
  0.0 54.0 jit_solution(16733825163855030509)
XLA Ops:
  0.6 1.7 %copy.8.codes = s32[512,64]{1,0:T(8,128)} copy(s32[512,64]{0,1:T(8,128)} %param.9) | data formatting | bytes 262144 | tf_op args[4]
  2.4 48.0 %shard_map.76 = (f32[256,1024]{1,0:T(8,128)}, f32[1,256]{1,0:T(1,128)}, f32[256,256]{1,0:T(8,128)}) custom-call(bf16[512,1024]{1,0:T(8,128)(2,1)} %emb.1, bf16[1024,1024]{1,0:T(8,128)(2,1)} %rot.1, bf16[8,1024]{1,0:T(8,128)(2,1)} %cent.1, s32[1,512]{1,0:T(1,128)} %bitcast.1, s32[512,64]{1,0:T(8,128)} %copy.8.codes), custom_call_target="tpu_custom_call" | custom-call | tf_op jit(solution)/shard_map/pallas_call | solution.py:334
  50.3 0.0 copy-start.1
  50.3 0.0 copy-start
  50.4 2.3 %copy.12 = f32[256,1024]{1,0:T(8,128)} copy(f32[256,1024]{1,0:T(8,128)} %get-tuple-element.6) | data formatting | bytes 2097152
  52.7 0.0 copy-done.1
  52.7 0.6 %copy.13 = f32[1,256]{1,0:T(1,128)} copy(f32[1,256]{1,0:T(1,128)S(1)} %copy-done.1) | data formatting | bytes 2048
  53.3 0.0 copy-done
  53.3 0.7 %copy.14 = f32[256,256]{1,0:T(8,128)} copy(f32[256,256]{1,0:T(8,128)S(1)} %copy-done) | data formatting | bytes 524288
Async XLA Ops:
  50.3 2.4 %copy-start.1 = (f32[1,256]{1,0:T(1,128)S(1)}, f32[1,256]{1,0:T(1,128)}, u32[]{:S(2)}) copy-start(f32[1,256]{1,0:T(1,128)} %get-tuple-element.7) | copy-start | bytes 3076
  50.3 2.9 %copy-start = (f32[256,256]{1,0:T(8,128)S(1)}, f32[256,256]{1,0:T(8,128)}, u32[]{:S(2)}) copy-start(f32[256,256]{1,0:T(8,128)} %get-tuple-element.8) | copy-start | bytes 786436

commit v3 on v2

--- a/solution.py
+++ b/solution.py
@@ -173,7 +173,27 @@
         ball[q, 0:K, lanes] = total
         return carry
 
-    lax.fori_loop(0, width // LANES, group_step, 0)
+    def quarter(k):
+        return lax.rem(dq + k, nq)
+
+    partner = (dq * 2 + 1 - dpar, s)
+    g3 = {}
+    def open_piece(h):
+        span = pl.ds(h * pr, pr)
+        total = gacc[span, :]
+        for k in range(nh - 1):
+            g2[k, h].wait_recv()
+            total = total + gr2[k, span, :].astype(f32)
+        split = total.reshape(nq, 2, cr, width)
+        for e in range(2):
+            gx[h, e] = split[:, e]
+            gs3[h, e] = split[:, e].astype(bf16)
+        g3[h] = send(gs3.at[h, 1 - dpar], gr3.at[h], partner)
+
+    steps = width // LANES
+    for h in range(PIECES):
+        lax.fori_loop(steps * h // PIECES, steps * (h + 1) // PIECES, group_step, 0)
+        open_piece(h)
     cpad = ball.shape[1] - K
     select_pad = (asg_row == lax.broadcasted_iota(jnp.int32, (cpad, rows), 0)).astype(f32).astype(bf16)
     for q in range(ns):
@@ -196,22 +216,6 @@
         else:
             bacc[...] = both
 
-    def quarter(k):
-        return lax.rem(dq + k, nq)
-
-    partner = (dq * 2 + 1 - dpar, s)
-    g3 = {}
-    for h in range(PIECES):
-        span = pl.ds(h * pr, pr)
-        total = gacc[span, :]
-        for k in range(nh - 1):
-            g2[k, h].wait_recv()
-            total = total + gr2[k, span, :].astype(f32)
-        split = total.reshape(nq, 2, cr, width)
-        for e in range(2):
-            gx[h, e] = split[:, e]
-            gs3[h, e] = split[:, e].astype(bf16)
-        g3[h] = send(gs3.at[h, 1 - dpar], gr3.at[h], partner)
     total = bacc[...]
     for k in range(nh - 1):
         b2[k].wait_recv()

time: 54.1 us -> 57.2 us (1.057)
  Pallas kernels: 48 us -> 51 us
    pallas_call x1, Pallas kernels: 48 us -> 51 us  [fused_per_device(): pl.pallas_call(functools.partial(kernel, ns, nd, total_rows), out_shape=(...]
where the time goes in v3:
time: 57.2 us; the launch traced here: 57.1 us
  Pallas kernels  51 us (89%)
  local copies, waits for them, and re-layouts  5.36 us (9%)
  between operations  0.66 us (1%)
    pallas_call x1, Pallas kernels, fused_per_device(): pl.pallas_call(functools.partial(kernel, ns, nd, total_rows), out_shape=(...  51 us
    unnamed x8, local copies, waits for them, and re-layouts  5.36 us

profile of v3, /device:TPU:0, one launch (start us, length us, event | category | flops | bytes accessed | tf_op | source)
XLA Modules:
  0.0 57.1 jit_solution(6244336312763552649)
XLA Ops:
  0.6 1.7 %copy.8.codes = s32[512,64]{1,0:T(8,128)} copy(s32[512,64]{0,1:T(8,128)} %param.9) | data formatting | bytes 262144 | tf_op args[4]
  2.4 51.0 %shard_map.76 = (f32[256,1024]{1,0:T(8,128)}, f32[1,256]{1,0:T(1,128)}, f32[256,256]{1,0:T(8,128)}) custom-call(bf16[512,1024]{1,0:T(8,128)(2,1)} %emb.1, bf16[1024,1024]{1,0:T(8,128)(2,1)} %rot.1, bf16[8,1024]{1,0:T(8,128)(2,1)} %cent.1, s32[1,512]{1,0:T(1,128)} %bitcast.1, s32[512,64]{1,0:T(8,128)} %copy.8.codes), custom_call_target="tpu_custom_call" | custom-call | tf_op jit(solution)/shard_map/pallas_call | solution.py:338
  53.4 0.0 copy-start.1
  53.4 0.0 copy-start
  53.4 2.3 %copy.12 = f32[256,1024]{1,0:T(8,128)} copy(f32[256,1024]{1,0:T(8,128)} %get-tuple-element.6) | data formatting | bytes 2097152
  55.8 0.0 copy-done.1
  55.8 0.6 copy.13
  56.4 0.0 copy-done
  56.4 0.7 %copy.14 = f32[256,256]{1,0:T(8,128)} copy(f32[256,256]{1,0:T(8,128)S(1)} %copy-done) | data formatting | bytes 524288
Async XLA Ops:
  53.4 2.4 %copy-start.1 = (f32[1,256]{1,0:T(1,128)S(1)}, f32[1,256]{1,0:T(1,128)}, u32[]{:S(2)}) copy-start(f32[1,256]{1,0:T(1,128)} %get-tuple-element.7) | copy-start | bytes 3076
  53.4 2.9 %copy-start = (f32[256,256]{1,0:T(8,128)S(1)}, f32[256,256]{1,0:T(8,128)}, u32[]{:S(2)}) copy-start(f32[256,256]{1,0:T(8,128)} %get-tuple-element.8) | copy-start | bytes 786436
